TPU v7x, 32 devices: a whole 2x2x4 slice. The times are simulated.
32 devices in a mesh: mat: 4 (over x, core), frac: 8 (over z, y).
Axes of the slice: x: 2, y: 2, z: 4, core: 2. Of those that a mesh axis runs over, the one named last changes fastest.
Arguments:
- pressure_start: float32 [64, 512, 256], P('mat', 'frac'), may hold values from -6 to 6
- face_trans: float32 [3, 64, 512, 256], P(None, 'mat', 'frac'), may hold values from 0.2 to 2
- cell_coef: float32 [64, 512, 256], P('mat', 'frac'), may hold values from 0.05 to 0.5
- matrix_source: float32 [64, 512, 256], P('mat', 'frac'), may hold values from -6 to 6
- mortar_owner: int32 [16384, 1], P(('mat', 'frac')), may hold values from 0 to 31; in each aligned block of 512 rows (0 to 511, 512 to 1023, ...) at most 32 rows name the same one
- mortar_cell: int32 [16384], P(('mat', 'frac')), may hold values from 0 to 262143
- mortar_frac: int32 [16384], P(('mat', 'frac')), may hold values from 0 to 8191
- mortar_kappa: float32 [16384], P(('mat', 'frac')), may hold values from 0.5 to 2
- tiles: float32 [64, 4, 128, 128], P('frac'), may hold values from -0.25 to 0.25
- tile_cols: int32 [64, 4], P('frac'), may hold values from 0 to 63
- frac_diag: float32 [8192], P('frac'), may hold values from 4 to 8
- frac_source: float32 [8192], P('frac'), may hold values from -6 to 6
- fracture_start: float32 [8192], P('frac'), may hold values from -6 to 6
Outputs:
- pressure: float32 [64, 512, 256], P('mat', 'frac')
- fracture: float32 [8192], P('frac')
- flux: float32 [16384], P(('mat', 'frac'))
Inputs may be any that keep to these rules, and one draw needn't show every extreme that they name: `mortar_owner`: among the 512 mortar cells of one device, at most 32 name the same owner, and in some devices some owner is named exactly 32 times.
All inputs are finite; a program needn't handle non-finite values.
Results may differ from a plain program's by a relative error of at most 0.00015.
Values sent between devices are 32-bit elements; how exact they have to be, the bound alone decides.
A program may use at most 128 MiB of HBM per device.

v0:
```python
import jax
import jax.numpy as jnp
from jax import lax
from jax.sharding import PartitionSpec as P

SWEEPS = 2
CG_ITERS = 3
OUTER = 2
relax_weight = 0.8


def shifted(value, axis, steps):
    count = lax.axis_size(axis)
    leading, last = (max(0, -steps), min(count, count - steps))
    return lax.ppermute(value, axis, [(source, source + steps) for source in range(leading, last)])


def with_halo(block, sides, width):
    for axis, dim in sides:
        count = lax.axis_size(axis)
        forward = [(i, i + 1) for i in range(count - 1)]
        backward = [(target, source) for source, target in forward]
        low = lax.ppermute(
            lax.slice_in_dim(block, block.shape[dim] - width, None, axis=dim), axis, forward
        )
        high = lax.ppermute(lax.slice_in_dim(block, 0, width, axis=dim), axis, backward)
        block = jnp.concatenate([low, block, high], axis=dim)
    return block


def shift_next(values, along):
    padding = [(0, 0)] * values.ndim
    padding[along] = (0, 1)
    return lax.slice_in_dim(jnp.pad(values, padding), 1, values.shape[along] + 1, axis=along)


def shift_prev(values, along):
    padding = [(0, 0)] * values.ndim
    padding[along] = (1, 0)
    return lax.slice_in_dim(jnp.pad(values, padding), 0, values.shape[along], axis=along)


def relax(padded, coef_part, source_part, inside):
    centre = padded[1:-1, 1:-1]
    tx_here = coef_part[0, 1:-1, 1:-1]
    tx_low = coef_part[0, :-2, 1:-1]
    ty_here = coef_part[1, 1:-1, 1:-1]
    ty_low = coef_part[1, 1:-1, :-2]
    tz_here = coef_part[2, 1:-1, 1:-1]
    tz_low = shift_prev(tz_here, 2)
    cell_part = coef_part[3, 1:-1, 1:-1]
    base_part = coef_part[4, 1:-1, 1:-1]
    diagonal = cell_part + tx_here + tx_low + ty_here + ty_low + tz_here + tz_low
    diagonal = jnp.where(inside, diagonal, 1.0)
    applied = (
        diagonal * centre
        - tx_here * padded[2:, 1:-1]
        - tx_low * padded[:-2, 1:-1]
        - ty_here * padded[1:-1, 2:]
        - ty_low * padded[1:-1, :-2]
        - tz_here * shift_next(centre, 2)
        - tz_low * shift_prev(centre, 2)
    )
    updated = centre + relax_weight * (base_part + source_part - applied) / diagonal
    return jnp.where(inside, updated, 0.0)


def body(
    pressure_start,
    face_trans,
    cell_coef,
    matrix_source,
    mortar_owner,
    mortar_cell,
    mortar_frac,
    mortar_kappa,
    tiles,
    tile_cols,
    frac_diag,
    frac_source,
    fracture_start,
):
    width_x, width_y, depth_z = pressure_start.shape
    cells = width_x * width_y * depth_z
    mat_count = lax.axis_size("mat")
    frac_count = lax.axis_size("frac")
    devices = mat_count * frac_count
    row_mat = lax.axis_index("mat")
    row_frac = lax.axis_index("frac")
    size_b = tiles.shape[2]
    coefs = jnp.concatenate([face_trans, cell_coef[None], matrix_source[None]], 0)
    lower_x = shifted(face_trans[0, -1], "mat", 1)
    lower_y = shifted(face_trans[1, :, -1], "frac", 1)
    coef_ext = jnp.pad(coefs, ((0, 0), (1, 1), (1, 1), (0, 0)))
    coef_ext = coef_ext.at[0, 0, 1:-1].set(lower_x)
    coef_ext = coef_ext.at[1, 1:-1, 0].set(lower_y)
    owner = mortar_owner[:, 0]
    mortar_count = owner.shape[0]
    capacity = max(2, 2 * mortar_count // devices)
    hits = (owner[:, None] == jnp.arange(devices, dtype=jnp.int32)[None, :]).astype(jnp.int32)
    ranks = jnp.cumsum(hits, axis=0)
    slot = jnp.sum(ranks * hits, axis=1) - 1
    place = owner * capacity + slot
    index_slots = (
        jnp.full((devices * capacity,), cells, jnp.int32)
        .at[place]
        .set(mortar_cell)
        .reshape(devices, capacity)
    )
    asked = lax.all_to_all(index_slots, ("mat", "frac"), split_axis=0, concat_axis=0, tiled=True)
    asked_safe = jnp.minimum(asked, cells - 1)

    def fracture_apply(vector):
        whole = lax.all_gather(vector, "frac", axis=0, tiled=True)
        blocks = whole.reshape(-1, size_b)
        forward = jnp.einsum(
            "rtij,rtj->ri", tiles, blocks[tile_cols], precision=lax.Precision.HIGHEST
        )
        backward = jnp.einsum(
            "rtij,ri->rtj", tiles, vector.reshape(-1, size_b), precision=lax.Precision.HIGHEST
        )
        spread = jnp.zeros_like(blocks).at[tile_cols.reshape(-1)].add(backward.reshape(-1, size_b))
        returned = lax.psum_scatter(spread, "frac", scatter_dimension=0, tiled=True)
        return frac_diag * vector + 0.5 * (forward + returned).reshape(-1)

    def two_products(residual, image):
        return lax.psum((jnp.sum(residual * residual), jnp.sum(residual * image)), "frac")

    def solve_fracture(fracture, target):
        residual = target - fracture_apply(fracture)
        image = fracture_apply(residual)
        norm_now, product = two_products(residual, image)
        alpha = norm_now / product
        direction, along_image = (residual, image)
        for step in range(CG_ITERS):
            fracture = fracture + alpha * direction
            residual = residual - alpha * along_image
            if step + 1 < CG_ITERS:
                image = fracture_apply(residual)
                norm_next, product = two_products(residual, image)
                ratio = norm_next / norm_now
                alpha = norm_next / (product - ratio * norm_next / alpha)
                direction = residual + ratio * direction
                along_image = image + ratio * along_image
                norm_now = norm_next
        return fracture

    pressure = pressure_start
    fracture = fracture_start
    flux = jnp.zeros(mortar_kappa.shape, jnp.float32)
    for outer_no in range(OUTER):
        local_values = pressure.reshape(-1)[asked_safe]
        returned = lax.all_to_all(
            local_values, ("mat", "frac"), split_axis=0, concat_axis=0, tiled=True
        )
        trace = returned.reshape(-1)[place]
        fracture_whole = lax.all_gather(fracture, "frac", axis=0, tiled=True)
        flux = mortar_kappa * (trace - fracture_whole[mortar_frac])
        landed = jax.ops.segment_sum(flux, mortar_frac, num_segments=fracture_whole.shape[0])
        summed = lax.psum(landed, ("mat", "frac"))
        load = lax.dynamic_slice_in_dim(summed, row_frac * fracture.shape[0], fracture.shape[0])
        fracture = solve_fracture(fracture, frac_source + load)
        flux_slots = (
            jnp.zeros((devices * capacity,), jnp.float32)
            .at[place]
            .set(flux)
            .reshape(devices, capacity)
        )
        arrived = lax.all_to_all(
            flux_slots, ("mat", "frac"), split_axis=0, concat_axis=0, tiled=True
        )
        source = jax.ops.segment_sum(
            arrived.reshape(-1), asked_safe.reshape(-1), num_segments=cells
        ).reshape(pressure.shape)
        for sweep_no in range(SWEEPS):
            padded = with_halo(pressure, (("mat", 0), ("frac", 1)), 1)
            global_x = row_mat * width_x - 0 + jnp.arange(width_x)
            global_y = row_frac * width_y - 0 + jnp.arange(width_y)
            keep_x = (global_x >= 0) & (global_x < width_x * mat_count)
            keep_y = (global_y >= 0) & (global_y < width_y * frac_count)
            pressure = relax(
                padded, coef_ext, source, (keep_x[:, None] & keep_y[None, :])[:, :, None]
            )
    return (pressure, fracture, flux)


def solution(mesh):
    in_specs = (
        P("mat", "frac", None),
        P(None, "mat", "frac", None),
        P("mat", "frac", None),
        P("mat", "frac", None),
        P(("mat", "frac"), None),
        P(("mat", "frac")),
        P(("mat", "frac")),
        P(("mat", "frac")),
        P("frac", None, None, None),
        P("frac", None),
        P("frac"),
        P("frac"),
        P("frac"),
    )
    out_specs = (P("mat", "frac", None), P("frac"), P(("mat", "frac")))
    return jax.shard_map(body, mesh=mesh, in_specs=in_specs, out_specs=out_specs, check_vma=False)
```

profile of v0, /device:TPU:0, one launch (start us, length us, event | category | flops | bytes accessed | tf_op | source)
XLA Modules:
  0.0 977.3 jit_solution(13991142482101642097)
XLA Ops:
  30.5 31.1 %all_gather.26 = f32[8192]{0:T(1024)S(1)} all-gather(f32[1024]{0:T(1024)} %param.29), channel_id=1, replica_groups=mesh['mat'=4,'frac'=8] {'frac'}, dimensions={0}, use_global_device_ids=true | all-gather | bytes 36864 | tf_op jit(solution)/shard_map/all_gather | solution.py:157
  83.4 37.4 %all-reduce.10 = f32[64,128]{1,0:T(8,128)S(1)} all-reduce(f32[64,128]{1,0:T(8,128)S(1)} %scatter_custom_fusion.4), channel_id=2, replica_groups=mesh['mat'=4,'frac'=8] {'frac'}, use_global_device_ids=true, to_apply=%region_9.10.clone | all-reduce | flops 8192 | bytes 65536
  138.0 40.6 %psum.98 = f32[8192]{0:T(1024)S(1)} all-reduce(f32[8192]{0:T(1024)S(1)} %scatter_custom_fusion.3), channel_id=1, replica_groups=mesh['mat'=4,'frac'=8] {'mat','frac'}, use_global_device_ids=true, to_apply=%region_7.8 | all-reduce | flops 8192 | bytes 65536 | tf_op jit(solution)/shard_map/psum | solution.py:160
  178.7 30.8 %all_gather.27 = f32[8192]{0:T(1024)S(1)} all-gather(f32[1024]{0:T(1024)S(1)} %fusion.134), channel_id=1, replica_groups=mesh['mat'=4,'frac'=8] {'frac'}, dimensions={0}, use_global_device_ids=true | all-gather | bytes 36864 | tf_op jit(solution)/shard_map/all_gather | solution.py:114
  213.7 36.8 %all-reduce.11 = f32[64,128]{1,0:T(8,128)S(1)} all-reduce(f32[64,128]{1,0:T(8,128)S(1)} %scatter_custom_fusion.5), channel_id=3, replica_groups=mesh['mat'=4,'frac'=8] {'frac'}, use_global_device_ids=true, to_apply=%region_13.14.clone | all-reduce | flops 8192 | bytes 65536
  251.2 17.8 %all-reduce.23 = (f32[]{:T(128)}, f32[]{:T(128)}) all-reduce(f32[]{:T(128)} %get-tuple-element.38, f32[]{:T(128)} %get-tuple-element.37), channel_id=1, replica_groups=mesh['mat'=4,'frac'=8] {'frac'}, use_global_device_ids=true, to_apply=%region_11.12 | all-reduce | flops 2 | bytes 16 | tf_op jit(solution)/shard_map/psum | solution.py:127
  270.3 30.6 %all_gather.28 = f32[8192]{0:T(1024)S(1)} all-gather(f32[1024]{0:T(1024)S(1)} %multiply_subtract_fusion.3), channel_id=1, replica_groups=mesh['mat'=4,'frac'=8] {'frac'}, dimensions={0}, use_global_device_ids=true | all-gather | bytes 36864 | tf_op jit(solution)/shard_map/all_gather | solution.py:114
  305.1 34.9 %all-reduce.12 = f32[64,128]{1,0:T(8,128)S(1)} all-reduce(f32[64,128]{1,0:T(8,128)S(1)} %scatter_custom_fusion.6), channel_id=4, replica_groups=mesh['mat'=4,'frac'=8] {'frac'}, use_global_device_ids=true, to_apply=%region_19.20.clone | all-reduce | flops 8192 | bytes 65536
  340.7 17.8 %all-reduce.22 = (f32[]{:T(128)}, f32[]{:T(128)}) all-reduce(f32[]{:T(128)} %get-tuple-element.36, f32[]{:T(128)} %get-tuple-element.35), channel_id=1, replica_groups=mesh['mat'=4,'frac'=8] {'frac'}, use_global_device_ids=true, to_apply=%region_17.18 | all-reduce | flops 2 | bytes 16 | tf_op jit(solution)/shard_map/psum | solution.py:127
  362.9 30.6 %all_gather.29 = f32[8192]{0:T(1024)S(1)} all-gather(f32[1024]{0:T(1024)S(1)} %multiply_subtract_fusion.2), channel_id=1, replica_groups=mesh['mat'=4,'frac'=8] {'frac'}, dimensions={0}, use_global_device_ids=true | all-gather | bytes 36864 | tf_op jit(solution)/shard_map/all_gather | solution.py:114
  397.8 34.9 %all-reduce.13 = f32[64,128]{1,0:T(8,128)S(1)} all-reduce(f32[64,128]{1,0:T(8,128)S(1)} %scatter_custom_fusion.7), channel_id=5, replica_groups=mesh['mat'=4,'frac'=8] {'frac'}, use_global_device_ids=true, to_apply=%region_25.26.clone | all-reduce | flops 8192 | bytes 65536
  433.3 17.8 %all-reduce.21 = (f32[]{:T(128)}, f32[]{:T(128)}) all-reduce(f32[]{:T(128)} %get-tuple-element.34, f32[]{:T(128)} %get-tuple-element.33), channel_id=1, replica_groups=mesh['mat'=4,'frac'=8] {'frac'}, use_global_device_ids=true, to_apply=%region_23.24 | all-reduce | flops 2 | bytes 16 | tf_op jit(solution)/shard_map/psum | solution.py:127
  454.9 30.6 %all_gather.30 = f32[8192]{0:T(1024)S(1)} all-gather(f32[1024]{0:T(1024)S(1)} %multiply_add_fusion.1), channel_id=1, replica_groups=mesh['mat'=4,'frac'=8] {'frac'}, dimensions={0}, use_global_device_ids=true | all-gather | bytes 36864 | tf_op jit(solution)/shard_map/all_gather | solution.py:157
  530.4 37.6 %all-reduce.14 = f32[64,128]{1,0:T(8,128)S(1)} all-reduce(f32[64,128]{1,0:T(8,128)S(1)} %scatter_custom_fusion.11), channel_id=6, replica_groups=mesh['mat'=4,'frac'=8] {'frac'}, use_global_device_ids=true, to_apply=%region_33.34.clone | all-reduce | flops 8192 | bytes 65536
  608.3 41.0 %psum.105 = f32[8192]{0:T(1024)S(1)} all-reduce(f32[8192]{0:T(1024)S(1)} %scatter_custom_fusion.10), channel_id=1, replica_groups=mesh['mat'=4,'frac'=8] {'mat','frac'}, use_global_device_ids=true, to_apply=%region_31.32 | all-reduce | flops 8192 | bytes 65536 | tf_op jit(solution)/shard_map/psum | solution.py:160
  649.3 30.6 %all_gather.31 = f32[8192]{0:T(1024)S(1)} all-gather(f32[1024]{0:T(1024)S(1)} %fusion.119), channel_id=1, replica_groups=mesh['mat'=4,'frac'=8] {'frac'}, dimensions={0}, use_global_device_ids=true | all-gather | bytes 36864 | tf_op jit(solution)/shard_map/all_gather | solution.py:114
  684.3 36.9 %all-reduce.15 = f32[64,128]{1,0:T(8,128)S(1)} all-reduce(f32[64,128]{1,0:T(8,128)S(1)} %scatter_custom_fusion.12), channel_id=7, replica_groups=mesh['mat'=4,'frac'=8] {'frac'}, use_global_device_ids=true, to_apply=%region_37.38.clone | all-reduce | flops 8192 | bytes 65536
  721.9 17.8 %all-reduce.20 = (f32[]{:T(128)}, f32[]{:T(128)}) all-reduce(f32[]{:T(128)} %get-tuple-element.32, f32[]{:T(128)} %get-tuple-element.31), channel_id=1, replica_groups=mesh['mat'=4,'frac'=8] {'frac'}, use_global_device_ids=true, to_apply=%region_35.36 | all-reduce | flops 2 | bytes 16 | tf_op jit(solution)/shard_map/psum | solution.py:127
  741.0 30.6 %all_gather.32 = f32[8192]{0:T(1024)S(1)} all-gather(f32[1024]{0:T(1024)S(1)} %multiply_subtract_fusion.1), channel_id=1, replica_groups=mesh['mat'=4,'frac'=8] {'frac'}, dimensions={0}, use_global_device_ids=true | all-gather | bytes 36864 | tf_op jit(solution)/shard_map/all_gather | solution.py:114
  776.0 34.9 %all-reduce.16 = f32[64,128]{1,0:T(8,128)S(1)} all-reduce(f32[64,128]{1,0:T(8,128)S(1)} %scatter_custom_fusion.13), channel_id=8, replica_groups=mesh['mat'=4,'frac'=8] {'frac'}, use_global_device_ids=true, to_apply=%region_43.44.clone | all-reduce | flops 8192 | bytes 65536
  811.5 17.8 %all-reduce.19 = (f32[]{:T(128)}, f32[]{:T(128)}) all-reduce(f32[]{:T(128)} %get-tuple-element.30, f32[]{:T(128)} %get-tuple-element.29), channel_id=1, replica_groups=mesh['mat'=4,'frac'=8] {'frac'}, use_global_device_ids=true, to_apply=%region_41.42 | all-reduce | flops 2 | bytes 16 | tf_op jit(solution)/shard_map/psum | solution.py:127
  834.0 30.6 %all_gather.33 = f32[8192]{0:T(1024)S(1)} all-gather(f32[1024]{0:T(1024)S(1)} %multiply_subtract_fusion), channel_id=1, replica_groups=mesh['mat'=4,'frac'=8] {'frac'}, dimensions={0}, use_global_device_ids=true | all-gather | bytes 36864 | tf_op jit(solution)/shard_map/all_gather | solution.py:114
  871.8 38.1 %all-reduce.17 = f32[64,128]{1,0:T(8,128)S(1)} all-reduce(f32[64,128]{1,0:T(8,128)S(1)} %scatter_custom_fusion.14), channel_id=9, replica_groups=mesh['mat'=4,'frac'=8] {'frac'}, use_global_device_ids=true, to_apply=%region_49.50.clone | all-reduce | flops 8192 | bytes 65536
  935.2 17.8 %all-reduce.18 = (f32[]{:T(128)}, f32[]{:T(128)}) all-reduce(f32[]{:T(128)} %get-tuple-element.28, f32[]{:T(128)} %get-tuple-element.27), channel_id=1, replica_groups=mesh['mat'=4,'frac'=8] {'frac'}, use_global_device_ids=true, to_apply=%region_47.48 | all-reduce | flops 2 | bytes 16 | tf_op jit(solution)/shard_map/psum | solution.py:127
  (229 shorter events, 229.9 us)
Async XLA Ops:
  2.3 498.6 %collective-permute-start = (f32[64,256]{1,0:T(8,128)}, f32[64,256]{1,0:T(8,128)S(1)}, u32[]{:S(2)}, u32[]{:S(2)}) collective-permute-start(f32[64,256]{1,0:T(8,128)} %slice_bitcast_fusion.7), channel_id=1, source_target_pairs={{0,8},{8,16},{16,24},{1,9},{9,17},{17,25},{2,10},{10,18},{18,26},{... | collective-permute-start | bytes 196616 | tf_op jit(solution)/shard_map/ppermute | solution.py:15
  5.7 480.3 %collective-permute-start.1 = (f32[16,256]{1,0:T(8,128)S(1)}, f32[16,256]{1,0:T(8,128)S(1)}, u32[]{:S(2)}, u32[]{:S(2)}) collective-permute-start(f32[16,256]{1,0:T(8,128)S(1)} %bitcast.415), channel_id=1, source_target_pairs={{0,1},{1,2},{2,3},{3,4},{4,5},{5,6},{6,7},{8,9},{9,10},{10,11},{11... | collective-permute-start | bytes 49160 | tf_op jit(solution)/shard_map/ppermute | solution.py:15
  11.5 485.1 %collective-permute-start.3 = (f32[1,64,256]{2,1,0:T(8,128)}, f32[1,64,256]{2,1,0:T(8,128)S(1)}, u32[]{:S(2)}, u32[]{:S(2)}) collective-permute-start(f32[1,64,256]{2,1,0:T(8,128)} %get-tuple-element.72), channel_id=1, source_target_pairs={{0,8},{8,16},{16,24},{1,9},{9,17},{17,25},{2,10},{10,18},{18,26},{... | collective-permute-start | bytes 196616 | tf_op jit(solution)/shard_map/ppermute | solution.py:23
  14.9 481.9 %collective-permute-start.2 = (f32[1,64,256]{2,1,0:T(8,128)}, f32[1,64,256]{2,1,0:T(8,128)S(1)}, u32[]{:S(2)}, u32[]{:S(2)}) collective-permute-start(f32[1,64,256]{2,1,0:T(8,128)} %get-tuple-element.71), channel_id=1, source_target_pairs={{8,0},{16,8},{24,16},{9,1},{17,9},{25,17},{10,2},{18,10},{26,18},{... | collective-permute-start | bytes 196616 | tf_op jit(solution)/shard_map/ppermute | solution.py:26
  23.1 47.8 %all-to-all-start = ((s32[32,1,32]{2,1,0:T(1,128)}), s32[32,1,32]{2,1,0:T(1,128)S(1)}, u32[]{:S(2)}, u32[]{:S(2)}) async-start(s32[32,1,32]{2,1,0:T(1,128)} %all_to_all.30), calls=%async_computation | async-start | bytes 32768 | tf_op jit(solution)/shard_map/all_to_all | solution.py:110
  77.9 47.4 %all-to-all-start.1 = ((f32[32,1,32]{2,1,0:T(1,128)}), f32[32,1,32]{2,1,0:T(1,128)S(1)}, u32[]{:S(2)}, u32[]{:S(2)}) async-start(f32[32,1,32]{2,1,0:T(1,128)} %all_to_all.32), calls=%async_computation.1 | async-start | bytes 32768 | tf_op jit(solution)/shard_map/all_to_all | solution.py:153
  125.3 361.5 %copy-start.23 = (s32[1024]{0:T(1024)}, s32[1024]{0:T(1024)S(1)}, u32[]{:S(2)}) copy-start(s32[1024]{0:T(1024)S(1)} %reshape.528) | copy-start | bytes 12292
  135.5 350.6 %all-to-all-start.2 = ((f32[32,1,32]{2,1,0:T(1,128)}), f32[32,1,32]{2,1,0:T(1,128)S(1)}, u32[]{:S(2)}, u32[]{:S(2)}) async-start(f32[32,1,32]{2,1,0:T(1,128)} %all_to_all.34), calls=%async_computation.2 | async-start | bytes 32768 | tf_op jit(solution)/shard_map/all_to_all | solution.py:169
  497.8 7.7 collective-permute-start.5
  499.5 5.9 collective-permute-start.4
  513.3 6.2 collective-permute-start.6
  514.6 4.9 collective-permute-start.7
  519.5 48.6 %collective-permute-start.9 = (f32[18,1,256]{2,1,0:T(1,128)S(1)}, f32[18,1,256]{2,1,0:T(1,128)S(1)}, u32[]{:S(2)}, u32[]{:S(2)}) collective-permute-start(f32[18,1,256]{2,1,0:T(1,128)S(1)} %get-tuple-element.62), channel_id=1, source_target_pairs={{0,1},{1,2},{2,3},{3,4},{4,5},{5,6},{6,7},{8,9},{9,10},{10,11},{11... | collective-permute-start | bytes 55304 | tf_op jit(solution)/shard_map/ppermute | solution.py:23
  524.0 44.0 %collective-permute-start.8 = (f32[18,1,256]{2,1,0:T(1,128)S(1)}, f32[18,1,256]{2,1,0:T(1,128)S(1)}, u32[]{:S(2)}, u32[]{:S(2)}) collective-permute-start(f32[18,1,256]{2,1,0:T(1,128)S(1)} %get-tuple-element.61), channel_id=1, source_target_pairs={{1,0},{2,1},{3,2},{4,3},{5,4},{6,5},{7,6},{9,8},{10,9},{11,10},{12... | collective-permute-start | bytes 55304 | tf_op jit(solution)/shard_map/ppermute | solution.py:26
  584.8 9.7 all-to-all-start.3
  588.3 278.8 %collective-permute-start.10 = (f32[1,64,256]{2,1,0:T(8,128)S(1)}, f32[1,64,256]{2,1,0:T(8,128)S(1)}, u32[]{:S(2)}, u32[]{:S(2)}) collective-permute-start(f32[1,64,256]{2,1,0:T(8,128)S(1)} %get-tuple-element.68), channel_id=1, source_target_pairs={{8,0},{16,8},{24,16},{9,1},{17,9},{25,17},{10,2},{18,10},{26,18},{... | collective-permute-start | bytes 196616 | tf_op jit(solution)/shard_map/ppermute | solution.py:26
  589.6 277.5 %collective-permute-start.11 = (f32[1,64,256]{2,1,0:T(8,128)S(1)}, f32[1,64,256]{2,1,0:T(8,128)S(1)}, u32[]{:S(2)}, u32[]{:S(2)}) collective-permute-start(f32[1,64,256]{2,1,0:T(8,128)S(1)} %get-tuple-element.67), channel_id=1, source_target_pairs={{0,8},{8,16},{16,24},{1,9},{9,17},{17,25},{2,10},{10,18},{18,26},{... | collective-permute-start | bytes 196616 | tf_op jit(solution)/shard_map/ppermute | solution.py:23
  604.3 305.6 %all-to-all-start.4 = ((f32[32,1,32]{2,1,0:T(1,128)}), f32[32,1,32]{2,1,0:T(1,128)S(1)}, u32[]{:S(2)}, u32[]{:S(2)}) async-start(f32[32,1,32]{2,1,0:T(1,128)} %all_to_all.38), calls=%async_computation.4 | async-start | bytes 32768 | tf_op jit(solution)/shard_map/all_to_all | solution.py:169
  867.1 53.6 %collective-permute-start.13 = (f32[18,1,256]{2,1,0:T(1,128)S(1)}, f32[18,1,256]{2,1,0:T(1,128)S(1)}, u32[]{:S(2)}, u32[]{:S(2)}) collective-permute-start(f32[18,1,256]{2,1,0:T(1,128)S(1)} %get-tuple-element.60), channel_id=1, source_target_pairs={{0,1},{1,2},{2,3},{3,4},{4,5},{5,6},{6,7},{8,9},{9,10},{10,11},{11... | collective-permute-start | bytes 55304 | tf_op jit(solution)/shard_map/ppermute | solution.py:23
  868.4 52.3 %collective-permute-start.12 = (f32[18,1,256]{2,1,0:T(1,128)S(1)}, f32[18,1,256]{2,1,0:T(1,128)S(1)}, u32[]{:S(2)}, u32[]{:S(2)}) collective-permute-start(f32[18,1,256]{2,1,0:T(1,128)S(1)} %get-tuple-element.59), channel_id=1, source_target_pairs={{1,0},{2,1},{3,2},{4,3},{5,4},{6,5},{7,6},{9,8},{10,9},{11,10},{12... | collective-permute-start | bytes 55304 | tf_op jit(solution)/shard_map/ppermute | solution.py:26
  930.3 26.8 %collective-permute-start.14 = (f32[1,64,256]{2,1,0:T(8,128)S(1)}, f32[1,64,256]{2,1,0:T(8,128)S(1)}, u32[]{:S(2)}, u32[]{:S(2)}) collective-permute-start(f32[1,64,256]{2,1,0:T(8,128)S(1)} %get-tuple-element.66), channel_id=1, source_target_pairs={{8,0},{16,8},{24,16},{9,1},{17,9},{25,17},{10,2},{18,10},{26,18},{... | collective-permute-start | bytes 196616 | tf_op jit(solution)/shard_map/ppermute | solution.py:26
  931.6 25.5 %collective-permute-start.15 = (f32[1,64,256]{2,1,0:T(8,128)S(1)}, f32[1,64,256]{2,1,0:T(8,128)S(1)}, u32[]{:S(2)}, u32[]{:S(2)}) collective-permute-start(f32[1,64,256]{2,1,0:T(8,128)S(1)} %get-tuple-element.65), channel_id=1, source_target_pairs={{0,8},{8,16},{16,24},{1,9},{9,17},{17,25},{2,10},{10,18},{18,26},{... | collective-permute-start | bytes 196616 | tf_op jit(solution)/shard_map/ppermute | solution.py:23
  958.0 5.8 collective-permute-start.17
  962.0 5.7 collective-permute-start.16
  (26 other events, 1407.7 us)
where the time goes:
time: 987 us; the launch traced here: 977 us
  blocking collectives  725 us (73%)
  other arithmetic  78.4 us (8%)
  starting transfers between devices  61.4 us (6%)
  local copies, waits for them, and re-layouts  60.8 us (6%)
  matrix products  23.6 us (2%)
  between operations  22 us (2%)
    unnamed x8, blocking collectives  291 us
    all_gather x6, blocking collectives, fracture_apply(): whole = lax.all_gather(vector, 'frac', axis=0, tiled=True)  184 us
    psum x6, blocking collectives, two_products(): lax.psum((jnp.sum(residual * residual), jnp.sum(residual * image)), 'frac')  107 us
    psum x2, blocking collectives, body(): summed = lax.psum(landed, ('mat', 'frac'))  81.6 us
    all_gather x2, blocking collectives, body(): fracture_whole = lax.all_gather(fracture, 'frac', axis=0, tiled=True)  61.7 us
    select_n x4, other arithmetic, relax(): return jnp.where(inside, updated, 0.0)  33.9 us
    ppermute x8, starting transfers between devices, with_halo(): lax.ppermute(lax.slice_in_dim(block, block.shape[dim] - width, None, axis...  24 us
  transfers between devices with their start and end apart: 23, of which 2 were waited for; matrix products, arithmetic and copies ran while one was open for 12% of the time, Pallas kernels for 0%

commit v1 on v0

--- a/solution.py
+++ b/solution.py
@@ -157,7 +157,7 @@
         fracture_whole = lax.all_gather(fracture, "frac", axis=0, tiled=True)
         flux = mortar_kappa * (trace - fracture_whole[mortar_frac])
         landed = jax.ops.segment_sum(flux, mortar_frac, num_segments=fracture_whole.shape[0])
-        summed = lax.psum(landed, ("mat", "frac"))
+        summed = jnp.sum(lax.all_gather(landed, ("mat", "frac")), axis=0)
         load = lax.dynamic_slice_in_dim(summed, row_frac * fracture.shape[0], fracture.shape[0])
         fracture = solve_fracture(fracture, frac_source + load)
         flux_slots = (

time: 987 us -> 924 us (0.936)
  blocking collectives: 725 us -> 635 us
  between operations: 22 us -> 35 us
    psum x2 -> x0, blocking collectives: 81.6 us -> none  [body(): summed = lax.psum(landed, ('mat', 'frac'))]
  transfers between devices with their start and end apart: 23 -> 25, of which waited for: 2 -> 3; matrix products, arithmetic and copies ran while one was open for 12% -> 16% of each run, Pallas kernels for 0% -> 0%
where the time goes in v1:
time: 924 us; the launch traced here: 913 us
  blocking collectives  635 us (69%)
  other arithmetic  79.9 us (9%)
  starting transfers between devices  68.6 us (7%)
  local copies, waits for them, and re-layouts  62.7 us (7%)
  between operations  35 us (4%)
  matrix products  23.6 us (3%)
    unnamed x8, blocking collectives  282 us
    all_gather x6, blocking collectives, fracture_apply(): whole = lax.all_gather(vector, 'frac', axis=0, tiled=True)  184 us
    psum x6, blocking collectives, two_products(): lax.psum((jnp.sum(residual * residual), jnp.sum(residual * image)), 'frac')  107 us
    all_gather x2, blocking collectives, body(): fracture_whole = lax.all_gather(fracture, 'frac', axis=0, tiled=True)  61.6 us
    select_n x4, other arithmetic, relax(): return jnp.where(inside, updated, 0.0)  33.4 us
    ppermute x8, starting transfers between devices, with_halo(): lax.ppermute(lax.slice_in_dim(block, block.shape[dim] - width, None, axis...  24.1 us
  transfers between devices with their start and end apart: 25, of which 3 were waited for; matrix products, arithmetic and copies ran while one was open for 16% of the time, Pallas kernels for 0%

profile of v1, /device:TPU:0, one launch (start us, length us, event | category | flops | bytes accessed | tf_op | source)
XLA Modules:
  0.0 912.6 jit_solution(9396328665915336029)
XLA Ops:
  55.5 31.0 %all_gather.38 = f32[8192]{0:T(1024)S(1)} all-gather(f32[1024]{0:T(1024)S(1)} %copy-done.12), channel_id=1, replica_groups=mesh['mat'=4,'frac'=8] {'frac'}, dimensions={0}, use_global_device_ids=true | all-gather | bytes 36864 | tf_op jit(solution)/shard_map/all_gather | solution.py:157
  184.2 37.4 %all-reduce.10 = f32[64,128]{1,0:T(8,128)S(1)} all-reduce(f32[64,128]{1,0:T(8,128)S(1)} %scatter_custom_fusion.4), channel_id=4, replica_groups=mesh['mat'=4,'frac'=8] {'frac'}, use_global_device_ids=true, to_apply=%region_9.10.clone | all-reduce | flops 8192 | bytes 65536
  230.1 30.6 %all_gather.41 = f32[8192]{0:T(1024)S(1)} all-gather(f32[1024]{0:T(1024)S(1)} %fusion.134), channel_id=1, replica_groups=mesh['mat'=4,'frac'=8] {'frac'}, dimensions={0}, use_global_device_ids=true | all-gather | bytes 36864 | tf_op jit(solution)/shard_map/all_gather | solution.py:114
  265.0 35.9 %all-reduce.11 = f32[64,128]{1,0:T(8,128)S(1)} all-reduce(f32[64,128]{1,0:T(8,128)S(1)} %scatter_custom_fusion.5), channel_id=5, replica_groups=mesh['mat'=4,'frac'=8] {'frac'}, use_global_device_ids=true, to_apply=%region_13.14.clone | all-reduce | flops 8192 | bytes 65536
  301.4 17.8 %all-reduce.23 = (f32[]{:T(128)}, f32[]{:T(128)}) all-reduce(f32[]{:T(128)} %get-tuple-element.38, f32[]{:T(128)} %get-tuple-element.37), channel_id=1, replica_groups=mesh['mat'=4,'frac'=8] {'frac'}, use_global_device_ids=true, to_apply=%region_11.12 | all-reduce | flops 2 | bytes 16 | tf_op jit(solution)/shard_map/psum | solution.py:127
  320.6 30.8 %all_gather.42 = f32[8192]{0:T(1024)S(1)} all-gather(f32[1024]{0:T(1024)S(1)} %multiply_subtract_fusion.3), channel_id=1, replica_groups=mesh['mat'=4,'frac'=8] {'frac'}, dimensions={0}, use_global_device_ids=true | all-gather | bytes 36864 | tf_op jit(solution)/shard_map/all_gather | solution.py:114
  355.6 34.9 %all-reduce.12 = f32[64,128]{1,0:T(8,128)S(1)} all-reduce(f32[64,128]{1,0:T(8,128)S(1)} %scatter_custom_fusion.6), channel_id=6, replica_groups=mesh['mat'=4,'frac'=8] {'frac'}, use_global_device_ids=true, to_apply=%region_19.20.clone | all-reduce | flops 8192 | bytes 65536
  391.2 17.8 %all-reduce.22 = (f32[]{:T(128)}, f32[]{:T(128)}) all-reduce(f32[]{:T(128)} %get-tuple-element.36, f32[]{:T(128)} %get-tuple-element.35), channel_id=1, replica_groups=mesh['mat'=4,'frac'=8] {'frac'}, use_global_device_ids=true, to_apply=%region_17.18 | all-reduce | flops 2 | bytes 16 | tf_op jit(solution)/shard_map/psum | solution.py:127
  413.4 30.6 %all_gather.43 = f32[8192]{0:T(1024)S(1)} all-gather(f32[1024]{0:T(1024)S(1)} %multiply_subtract_fusion.2), channel_id=1, replica_groups=mesh['mat'=4,'frac'=8] {'frac'}, dimensions={0}, use_global_device_ids=true | all-gather | bytes 36864 | tf_op jit(solution)/shard_map/all_gather | solution.py:114
  448.2 34.9 %all-reduce.13 = f32[64,128]{1,0:T(8,128)S(1)} all-reduce(f32[64,128]{1,0:T(8,128)S(1)} %scatter_custom_fusion.7), channel_id=7, replica_groups=mesh['mat'=4,'frac'=8] {'frac'}, use_global_device_ids=true, to_apply=%region_25.26.clone | all-reduce | flops 8192 | bytes 65536
  483.8 17.8 %all-reduce.21 = (f32[]{:T(128)}, f32[]{:T(128)}) all-reduce(f32[]{:T(128)} %get-tuple-element.34, f32[]{:T(128)} %get-tuple-element.33), channel_id=1, replica_groups=mesh['mat'=4,'frac'=8] {'frac'}, use_global_device_ids=true, to_apply=%region_23.24 | all-reduce | flops 2 | bytes 16 | tf_op jit(solution)/shard_map/psum | solution.py:127
  505.3 30.6 %all_gather.44 = f32[8192]{0:T(1024)S(1)} all-gather(f32[1024]{0:T(1024)S(1)} %multiply_add_fusion.1), channel_id=1, replica_groups=mesh['mat'=4,'frac'=8] {'frac'}, dimensions={0}, use_global_device_ids=true | all-gather | bytes 36864 | tf_op jit(solution)/shard_map/all_gather | solution.py:157
  564.0 8.8 broadcast_select_fusion
  585.0 36.7 %all-reduce.14 = f32[64,128]{1,0:T(8,128)S(1)} all-reduce(f32[64,128]{1,0:T(8,128)S(1)} %scatter_custom_fusion.11), channel_id=8, replica_groups=mesh['mat'=4,'frac'=8] {'frac'}, use_global_device_ids=true, to_apply=%region_33.34.clone | all-reduce | flops 8192 | bytes 65536
  621.7 9.1 fusion.74
  632.3 30.6 %all_gather.47 = f32[8192]{0:T(1024)S(1)} all-gather(f32[1024]{0:T(1024)S(1)} %fusion.119), channel_id=1, replica_groups=mesh['mat'=4,'frac'=8] {'frac'}, dimensions={0}, use_global_device_ids=true | all-gather | bytes 36864 | tf_op jit(solution)/shard_map/all_gather | solution.py:114
  667.2 33.0 %all-reduce.15 = f32[64,128]{1,0:T(8,128)S(1)} all-reduce(f32[64,128]{1,0:T(8,128)S(1)} %scatter_custom_fusion.12), channel_id=9, replica_groups=mesh['mat'=4,'frac'=8] {'frac'}, use_global_device_ids=true, to_apply=%region_37.38.clone | all-reduce | flops 8192 | bytes 65536
  700.8 17.8 %all-reduce.20 = (f32[]{:T(128)}, f32[]{:T(128)}) all-reduce(f32[]{:T(128)} %get-tuple-element.32, f32[]{:T(128)} %get-tuple-element.31), channel_id=1, replica_groups=mesh['mat'=4,'frac'=8] {'frac'}, use_global_device_ids=true, to_apply=%region_35.36 | all-reduce | flops 2 | bytes 16 | tf_op jit(solution)/shard_map/psum | solution.py:127
  720.0 30.8 %all_gather.48 = f32[8192]{0:T(1024)S(1)} all-gather(f32[1024]{0:T(1024)S(1)} %multiply_subtract_fusion.1), channel_id=1, replica_groups=mesh['mat'=4,'frac'=8] {'frac'}, dimensions={0}, use_global_device_ids=true | all-gather | bytes 36864 | tf_op jit(solution)/shard_map/all_gather | solution.py:114
  755.1 34.9 %all-reduce.16 = f32[64,128]{1,0:T(8,128)S(1)} all-reduce(f32[64,128]{1,0:T(8,128)S(1)} %scatter_custom_fusion.13), channel_id=10, replica_groups=mesh['mat'=4,'frac'=8] {'frac'}, use_global_device_ids=true, to_apply=%region_43.44.clone | all-reduce | flops 8192 | bytes 65536
  790.6 17.8 %all-reduce.19 = (f32[]{:T(128)}, f32[]{:T(128)}) all-reduce(f32[]{:T(128)} %get-tuple-element.30, f32[]{:T(128)} %get-tuple-element.29), channel_id=1, replica_groups=mesh['mat'=4,'frac'=8] {'frac'}, use_global_device_ids=true, to_apply=%region_41.42 | all-reduce | flops 2 | bytes 16 | tf_op jit(solution)/shard_map/psum | solution.py:127
  812.8 30.6 %all_gather.49 = f32[8192]{0:T(1024)S(1)} all-gather(f32[1024]{0:T(1024)S(1)} %multiply_subtract_fusion), channel_id=1, replica_groups=mesh['mat'=4,'frac'=8] {'frac'}, dimensions={0}, use_global_device_ids=true | all-gather | bytes 36864 | tf_op jit(solution)/shard_map/all_gather | solution.py:114
  847.7 34.9 %all-reduce.17 = f32[64,128]{1,0:T(8,128)S(1)} all-reduce(f32[64,128]{1,0:T(8,128)S(1)} %scatter_custom_fusion.14), channel_id=11, replica_groups=mesh['mat'=4,'frac'=8] {'frac'}, use_global_device_ids=true, to_apply=%region_49.50.clone | all-reduce | flops 8192 | bytes 65536
  883.2 17.8 %all-reduce.18 = (f32[]{:T(128)}, f32[]{:T(128)}) all-reduce(f32[]{:T(128)} %get-tuple-element.28, f32[]{:T(128)} %get-tuple-element.27), channel_id=1, replica_groups=mesh['mat'=4,'frac'=8] {'frac'}, use_global_device_ids=true, to_apply=%region_47.48 | all-reduce | flops 2 | bytes 16 | tf_op jit(solution)/shard_map/psum | solution.py:127
  (227 shorter events, 224.8 us)
Async XLA Ops:
  8.2 117.0 %collective-permute-start = (f32[64,256]{1,0:T(8,128)S(1)}, f32[64,256]{1,0:T(8,128)S(1)}, u32[]{:S(2)}, u32[]{:S(2)}) collective-permute-start(f32[64,256]{1,0:T(8,128)S(1)} %slice_bitcast_fusion.7), channel_id=1, source_target_pairs={{0,8},{8,16},{16,24},{1,9},{9,17},{17,25},{2,10},{10,18},{18,26},{... | collective-permute-start | bytes 196616 | tf_op jit(solution)/shard_map/ppermute | solution.py:15
  11.5 95.6 %collective-permute-start.1 = (f32[16,256]{1,0:T(8,128)S(1)}, f32[16,256]{1,0:T(8,128)S(1)}, u32[]{:S(2)}, u32[]{:S(2)}) collective-permute-start(f32[16,256]{1,0:T(8,128)S(1)} %bitcast.415), channel_id=1, source_target_pairs={{0,1},{1,2},{2,3},{3,4},{4,5},{5,6},{6,7},{8,9},{9,10},{10,11},{11... | collective-permute-start | bytes 49160 | tf_op jit(solution)/shard_map/ppermute | solution.py:15
  17.3 101.9 %collective-permute-start.3 = (f32[1,64,256]{2,1,0:T(8,128)}, f32[1,64,256]{2,1,0:T(8,128)S(1)}, u32[]{:S(2)}, u32[]{:S(2)}) collective-permute-start(f32[1,64,256]{2,1,0:T(8,128)} %get-tuple-element.72), channel_id=1, source_target_pairs={{0,8},{8,16},{16,24},{1,9},{9,17},{17,25},{2,10},{10,18},{18,26},{... | collective-permute-start | bytes 196616 | tf_op jit(solution)/shard_map/ppermute | solution.py:23
  20.7 98.7 %collective-permute-start.2 = (f32[1,64,256]{2,1,0:T(8,128)}, f32[1,64,256]{2,1,0:T(8,128)S(1)}, u32[]{:S(2)}, u32[]{:S(2)}) collective-permute-start(f32[1,64,256]{2,1,0:T(8,128)} %get-tuple-element.71), channel_id=1, source_target_pairs={{8,0},{16,8},{24,16},{9,1},{17,9},{25,17},{10,2},{18,10},{26,18},{... | collective-permute-start | bytes 196616 | tf_op jit(solution)/shard_map/ppermute | solution.py:26
  28.9 13.8 %all-to-all-start = ((s32[32,1,32]{2,1,0:T(1,128)}), s32[32,1,32]{2,1,0:T(1,128)S(1)}, u32[]{:S(2)}, u32[]{:S(2)}) async-start(s32[32,1,32]{2,1,0:T(1,128)} %all_to_all.30), calls=%async_computation | async-start | bytes 32768 | tf_op jit(solution)/shard_map/all_to_all | solution.py:110
  49.7 40.0 %all-to-all-start.1 = ((f32[32,1,32]{2,1,0:T(1,128)}), f32[32,1,32]{2,1,0:T(1,128)S(1)}, u32[]{:S(2)}, u32[]{:S(2)}) async-start(f32[32,1,32]{2,1,0:T(1,128)} %all_to_all.32), calls=%async_computation.1 | async-start | bytes 32768 | tf_op jit(solution)/shard_map/all_to_all | solution.py:153
  96.3 12.5 %all-to-all-start.2 = ((f32[32,1,32]{2,1,0:T(1,128)}), f32[32,1,32]{2,1,0:T(1,128)S(1)}, u32[]{:S(2)}, u32[]{:S(2)}) async-start(f32[32,1,32]{2,1,0:T(1,128)} %all_to_all.34), calls=%async_computation.2 | async-start | bytes 32768 | tf_op jit(solution)/shard_map/all_to_all | solution.py:169
  101.8 126.8 %all-gather.5.cloned.1.call-start = ((), (), s32[]{:S(2)}) async-start(), calls=%async_computation.5 | async-start | bytes 1081344 | tf_op jit(solution)/shard_map/all_gather | solution.py:160
  121.0 8.7 collective-permute-start.5
  123.8 5.9 collective-permute-start.4
  137.2 6.4 collective-permute-start.6
  138.5 5.1 collective-permute-start.7
  143.7 7.2 collective-permute-start.9
  148.2 6.2 collective-permute-start.8
  163.7 62.2 %collective-permute-start.10 = (f32[1,64,256]{2,1,0:T(8,128)S(1)}, f32[1,64,256]{2,1,0:T(8,128)S(1)}, u32[]{:S(2)}, u32[]{:S(2)}) collective-permute-start(f32[1,64,256]{2,1,0:T(8,128)S(1)} %get-tuple-element.68), channel_id=1, source_target_pairs={{8,0},{16,8},{24,16},{9,1},{17,9},{25,17},{10,2},{18,10},{26,18},{... | collective-permute-start | bytes 196616 | tf_op jit(solution)/shard_map/ppermute | solution.py:26
  165.0 60.9 %collective-permute-start.11 = (f32[1,64,256]{2,1,0:T(8,128)S(1)}, f32[1,64,256]{2,1,0:T(8,128)S(1)}, u32[]{:S(2)}, u32[]{:S(2)}) collective-permute-start(f32[1,64,256]{2,1,0:T(8,128)S(1)} %get-tuple-element.67), channel_id=1, source_target_pairs={{0,8},{8,16},{16,24},{1,9},{9,17},{17,25},{2,10},{10,18},{18,26},{... | collective-permute-start | bytes 196616 | tf_op jit(solution)/shard_map/ppermute | solution.py:23
  177.4 45.5 %all-to-all-start.3 = ((f32[32,1,32]{2,1,0:T(1,128)}), f32[32,1,32]{2,1,0:T(1,128)S(1)}, u32[]{:S(2)}, u32[]{:S(2)}) async-start(f32[32,1,32]{2,1,0:T(1,128)} %all_to_all.36), calls=%async_computation.3 | async-start | bytes 32768 | tf_op jit(solution)/shard_map/all_to_all | solution.py:153
  225.9 338.0 %collective-permute-start.13 = (f32[18,1,256]{2,1,0:T(1,128)S(1)}, f32[18,1,256]{2,1,0:T(1,128)S(1)}, u32[]{:S(2)}, u32[]{:S(2)}) collective-permute-start(f32[18,1,256]{2,1,0:T(1,128)S(1)} %get-tuple-element.60), channel_id=1, source_target_pairs={{0,1},{1,2},{2,3},{3,4},{4,5},{5,6},{6,7},{8,9},{9,10},{10,11},{11... | collective-permute-start | bytes 55304 | tf_op jit(solution)/shard_map/ppermute | solution.py:23
  227.2 336.7 %collective-permute-start.12 = (f32[18,1,256]{2,1,0:T(1,128)S(1)}, f32[18,1,256]{2,1,0:T(1,128)S(1)}, u32[]{:S(2)}, u32[]{:S(2)}) collective-permute-start(f32[18,1,256]{2,1,0:T(1,128)S(1)} %get-tuple-element.59), channel_id=1, source_target_pairs={{1,0},{2,1},{3,2},{4,3},{5,4},{6,5},{7,6},{9,8},{10,9},{11,10},{12... | collective-permute-start | bytes 55304 | tf_op jit(solution)/shard_map/ppermute | solution.py:26
  542.5 10.4 %all-to-all-start.4 = ((f32[32,1,32]{2,1,0:T(1,128)}), f32[32,1,32]{2,1,0:T(1,128)S(1)}, u32[]{:S(2)}, u32[]{:S(2)}) async-start(f32[32,1,32]{2,1,0:T(1,128)} %all_to_all.38), calls=%async_computation.4 | async-start | bytes 32768 | tf_op jit(solution)/shard_map/all_to_all | solution.py:169
  545.8 85.0 %all-gather.7.cloned.1.call-start = ((), (), s32[]{:S(2)}) async-start(), calls=%async_computation.6 | async-start | bytes 1081344 | tf_op jit(solution)/shard_map/all_gather | solution.py:160
  572.8 6.2 collective-permute-start.14
  579.0 42.7 %collective-permute-start.17 = (f32[18,1,256]{2,1,0:T(1,128)S(1)}, f32[18,1,256]{2,1,0:T(1,128)S(1)}, u32[]{:S(2)}, u32[]{:S(2)}) collective-permute-start(f32[18,1,256]{2,1,0:T(1,128)S(1)} %get-tuple-element.58), channel_id=1, source_target_pairs={{0,1},{1,2},{2,3},{3,4},{4,5},{5,6},{6,7},{8,9},{9,10},{10,11},{11... | collective-permute-start | bytes 55304 | tf_op jit(solution)/shard_map/ppermute | solution.py:23
  581.8 39.9 %collective-permute-start.16 = (f32[18,1,256]{2,1,0:T(1,128)S(1)}, f32[18,1,256]{2,1,0:T(1,128)S(1)}, u32[]{:S(2)}, u32[]{:S(2)}) collective-permute-start(f32[18,1,256]{2,1,0:T(1,128)S(1)} %get-tuple-element.57), channel_id=1, source_target_pairs={{1,0},{2,1},{3,2},{4,3},{5,4},{6,5},{7,6},{9,8},{10,9},{11,10},{12... | collective-permute-start | bytes 55304 | tf_op jit(solution)/shard_map/ppermute | solution.py:26
  (23 other events, 596.4 us)
Sparse Core Ops, SparseCore 0:
  107.2 55.3 all-gather.4
  550.5 55.2 all-gather.6
